TPU v7x, 32 devices: a whole 2x2x4 slice. The times are simulated.
32 devices in a mesh: dp: 2 (over x), tp: 16 (over y, z, core).
Axes of the slice: x: 2, y: 2, z: 4, core: 2. Of those that a mesh axis runs over, the one named last changes fastest.
Arguments:
- x: bfloat16 [256, 8192], P('dp'), parts along dimension 0
- w_gate: bfloat16 [8192, 32768], P(None, 'tp')
- w_up: bfloat16 [8192, 32768], P(None, 'tp')
- w_down: bfloat16 [32768, 8192], P('tp')
Outputs:
- output: bfloat16 [256, 8192], P('dp'), parts along dimension 0
There are 2 independent parts. A program takes and returns all parts, laid end to end along the dimension named above; an argument that names none is the same for every part.
All inputs are finite; a program needn't handle non-finite values.
Results may differ from a plain program's by a relative error of at most 0.016.
Values are sent between devices in bfloat16 or wider.
A program may use at most 2 GiB of HBM per device.

v0:
```python
import jax
import jax.numpy as jnp
from jax import lax
from jax.sharding import PartitionSpec as P


def solution(mesh):
    def step(x, w_gate, w_up, w_down):
        gate = jnp.dot(x, w_gate, preferred_element_type=jnp.float32)
        up = jnp.dot(x, w_up, preferred_element_type=jnp.float32)
        hidden = (jax.nn.silu(gate) * up).astype(jnp.bfloat16)
        term = jnp.dot(hidden, w_down, preferred_element_type=jnp.float32).astype(jnp.bfloat16)
        return lax.psum(term, "tp")

    return jax.shard_map(
        step,
        mesh=mesh,
        in_specs=(P("dp", None), P(None, "tp"), P(None, "tp"), P("tp", None)),
        out_specs=P("dp", None),
        check_vma=False,
    )
```

profile of v0, /device:TPU:0, one launch (start us, length us, event | category | flops | bytes accessed | tf_op | source)
XLA Modules:
  0.0 156.0 jit_solution(11849132639869667812)
XLA Ops:
  6.5 0.0 copy-start
  6.5 0.0 all-reduce.2.cloned.1.call-start
  6.5 1.6 %copy-done = bf16[128,8192]{1,0:T(8,128)(2,1)S(1)} copy-done((bf16[128,8192]{1,0:T(8,128)(2,1)S(1)}, bf16[128,8192]{1,0:T(8,128)(2,1)}, u32[]{:S(2)}) %copy-start) | copy-done | bytes 2097176
  8.1 12.9 %fusion.8 = f32[128,2048]{1,0:T(8,128)S(1)} fusion(bf16[128,8192]{1,0:T(8,128)(2,1)S(1)} %copy-done, bf16[8192,2048]{1,0:T(8,128)(2,1)} %param.5), kind=kOutput, calls=%fused_computation.10 | convolution fusion | flops 4294967296 | bytes 36700160 | tf_op jit(solution)/shard_map/dot_general | solution.py:9
  21.0 24.5 %convolution_convert_fusion = bf16[128,8192]{1,0:T(8,128)(2,1)} fusion(bf16[2048,8192]{1,0:T(8,128)(2,1)} %param.7, bf16[128,8192]{1,0:T(8,128)(2,1)S(1)} %copy-done, bf16[8192,2048]{1,0:T(8,128)(2,1)} %param.6, f32[128,2048]{1,0:T(8,128)S(1)} %fusion.8), kind=kOutput, calls=%fused_computation | convolution fusion | flops 8592556032 | bytes 72351744 | tf_op jit(solution)/shard_map/dot_general | solution.py:12
  45.5 0.0 all-reduce.2.cloned.1.call-update
  45.5 100.6 %all-reduce.2.cloned.1.call-done = bf16[128,8192]{1,0:T(8,128)(2,1)} async-done(((bf16[128,8192]{1,0:T(8,128)(2,1)}), bf16[128,8192]{1,0:T(8,128)(2,1)}) %all-reduce.2.cloned.1.call-update) | async-done | bytes 2097168 | tf_op jit(solution)/shard_map/psum | solution.py:13
  146.1 3.1 %copy.6 = bf16[128,8192]{1,0:T(8,128)(2,1)} copy(bf16[128,8192]{1,0:T(8,128)(2,1)} %all-reduce.2.cloned.1.call-done) | data formatting | bytes 4194304
Async XLA Ops:
  6.5 1.6 %copy-start = (bf16[128,8192]{1,0:T(8,128)(2,1)S(1)}, bf16[128,8192]{1,0:T(8,128)(2,1)}, u32[]{:S(2)}) copy-start(bf16[128,8192]{1,0:T(8,128)(2,1)} %param.4) | copy-start | bytes 6291460
  6.5 139.5 %all-reduce.2.cloned.1.call-start = ((), (), s32[]{:S(2)}) async-start(), calls=%async_computation | async-start | bytes 4194304 | tf_op jit(solution)/shard_map/psum | solution.py:13
Sparse Core Ops, SparseCore 0:
  45.6 100.3 all-reduce.1
where the time goes:
time: 156 us
  waiting for transfers between devices  101 us (65%)
  matrix products  37.4 us (24%)
  between operations  13.4 us (9%)
  local copies, waits for them, and re-layouts  4.68 us (3%)
    psum x1, waiting for transfers between devices, step(): return lax.psum(term, 'tp')  101 us
    dot_general x1, matrix products, step(): jnp.dot(hidden, w_down, preferred_element_type=jnp.float32)  24.5 us
    dot_general x1, matrix products, step(): gate = jnp.dot(x, w_gate, preferred_element_type=jnp.float32)  12.9 us
    unnamed x3, local copies, waits for them, and re-layouts  4.68 us
  transfers between devices with their start and end apart: 1, of which 1 were waited for; matrix products, arithmetic and copies ran while one was open for 0% of the time, Pallas kernels for 0%

commit v1 on v0

v1 whole, which is shorter than its diff:
```python
import functools

import jax
import jax.numpy as jnp
from jax import lax
from jax.experimental import pallas as pl
from jax.experimental.pallas import tpu as pltpu
from jax.sharding import PartitionSpec as P

MESH = pl.DeviceIdType.MESH
ROWS = 128
TK = 2048
TN = 512
SLOTS = 14
CORE, Y1, ZZ, ZY, MZ, MY, YZ, FYE, FYY, FZM, FZA, FZB, SY0, SY1, SZ0, SZ1 = range(16)


def kernel(x_hbm, wg_hbm, wu_hbm, wd_hbm, out, xv, wbuf, acc_g, acc_u, h, total,
           cs, cr, ys, yr, zzs, zzr, zys, zyr, mzs, mzr, mys, myr, yzs, yzr,
           xsem, wsem, ssem, rsem):
    dp = lax.axis_index("dp")
    tp = lax.axis_index("tp")
    c = lax.rem(tp, 2)
    z = lax.rem(tp // 2, 4)
    y = tp // 8
    half = z // 2
    inner = (z + 1) // 2 == 1
    ends = jnp.logical_not(inner)
    ff = wg_hbm.shape[1]
    d = wd_hbm.shape[1]
    kx = wg_hbm.shape[0] // TK
    nb = ff // TN
    n_up = 2 * kx * nb
    n_chunks = d // (2 * TN)
    n_steps = n_up + 2 * n_chunks

    def dev(yy, zz, cc):
        return (dp, (yy * 4 + zz) * 2 + cc)

    sib = dev(y, z, 1 - c)
    ynb = dev(1 - y, z, c)
    znb = dev(y, z + 1 - 2 * lax.rem(z, 2), c)
    mid = dev(y, 3 - z, c)

    barrier = pltpu.get_barrier_semaphore()
    for nbr in (sib, ynb, znb):
        pl.semaphore_signal(barrier, inc=1, device_id=nbr, device_id_type=MESH)

    @pl.when(inner)
    def _():
        pl.semaphore_signal(barrier, inc=1, device_id=mid, device_id_type=MESH)

    def tile_copy(ref, k, n, s):
        slot = lax.rem(s, SLOTS)
        return pltpu.make_async_copy(
            ref.at[pl.ds(k * TK, TK), pl.ds(n * TN, TN)], wbuf.at[slot], wsem.at[slot])

    def fetch_up(it):
        b, k = it // kx, lax.rem(it, kx)
        tile_copy(wg_hbm, k, b, 2 * it).start()
        tile_copy(wu_hbm, k, b, 2 * it + 1).start()

    def fetch_down(i):
        tile_copy(wd_hbm, 0, 2 * i, n_up + 2 * i).start()
        tile_copy(wd_hbm, 0, 2 * i + 1, n_up + 2 * i + 1).start()

    def fetch(it):
        @pl.when(it < kx * nb)
        def _():
            fetch_up(it)

        @pl.when(jnp.logical_and(it >= kx * nb, it < n_steps // 2))
        def _():
            fetch_down(it - kx * nb)

    def wait_tile(s):
        slot = lax.rem(s, SLOTS)
        pltpu.make_async_copy(wd_hbm.at[pl.ds(0, TK), pl.ds(0, TN)], wbuf.at[slot], wsem.at[slot]).wait()
        return slot

    def x_copy(k):
        return pltpu.make_async_copy(
            x_hbm.at[:, pl.ds(k * TK, TK)], xv.at[:, pl.ds(k * TK, TK)], xsem.at[k])

    for k in range(kx):
        x_copy(k).start()
        if k < SLOTS // 2 - 1:
            fetch_up(k)
    for k in range(kx, SLOTS // 2 - 1):
        fetch_up(k)

    @pl.loop(0, kx * nb)
    def _(it):
        b, k = it // kx, lax.rem(it, kx)
        fetch(it + SLOTS // 2 - 1)

        @pl.when(it < kx)
        def _():
            x_copy(k).wait()

        xk = xv[:, pl.ds(pl.multiple_of(k * TK, TK), TK)]

        @pl.when(k == 0)
        def _():
            acc_g[...] = jnp.zeros_like(acc_g)
            acc_u[...] = jnp.zeros_like(acc_u)

        slot = wait_tile(2 * it)
        acc_g[...] += jnp.dot(xk, wbuf[slot], preferred_element_type=jnp.float32)
        slot = wait_tile(2 * it + 1)
        acc_u[...] += jnp.dot(xk, wbuf[slot], preferred_element_type=jnp.float32)

        @pl.when(k == kx - 1)
        def _():
            h[:, pl.ds(pl.multiple_of(b * TN, TN), TN)] = (
                jax.nn.silu(acc_g[...]) * acc_u[...]).astype(jnp.bfloat16)

    @pl.when(inner)
    def _():
        pl.semaphore_wait(barrier, 4)

    @pl.when(ends)
    def _():
        pl.semaphore_wait(barrier, 3)

    def send(kind, k, src, dst, to):
        return pltpu.make_async_remote_copy(
            src_ref=src, dst_ref=dst, send_sem=ssem.at[kind, k], recv_sem=rsem.at[kind, k],
            device_id=to, device_id_type=MESH)

    rc = 64 * c
    ry, ry_other = rc + 32 * y, rc + 32 * (1 - y)
    rz, rz_other = rc + 32 * half, rc + 32 * (1 - half)

    def col(k, part):
        return pl.ds(pl.multiple_of(k * 2 * TN + part * TN, TN), TN)

    def rows(r, n):
        return pl.ds(pl.multiple_of(r, 32), n)

    def o(k, part, r):
        return out.at[rows(r, 32), col(k, part)]

    CY, CZ = pl.ds(0, TN), pl.ds(TN, TN)

    def f32(v):
        return v.astype(jnp.float32)

    def bf16(v):
        return v.astype(jnp.bfloat16)

    def core_send(k):
        return send(CORE, k, cs.at[k], cr.at[k], sib)

    def y1_send(k):
        return send(Y1, k, ys.at[k], yr.at[k], ynb)

    def zz_send(k):
        return send(ZZ, k, zzs.at[k], zzr.at[k], znb)

    def zy_send(k):
        return send(ZY, k, zys.at[k], zyr.at[k], znb)

    def mz_send(k):
        return send(MZ, k, mzs.at[k], mzr.at[k], mid)

    def my_send(k):
        return send(MY, k, mys.at[k], myr.at[k], mid)

    def yz_send(k):
        return send(YZ, k, yzs.at[k], yzr.at[k], ynb)

    def final(kind, k, part, r, to):
        return send(kind, k, o(k, part, r), o(k, part, r), to)

    def compute(k):
        for part in range(2):
            slot = wait_tile(n_up + 2 * k + part)
            total[k, :, part * TN:(part + 1) * TN] = jnp.dot(
                h[...], wbuf[slot], preferred_element_type=jnp.float32)
        cs[k] = bf16(total[k, rows(64 - rc, 64), :])
        core_send(k).start()

    def stage1(k):
        core_send(k).wait_recv()
        total[k, rows(rc, 64), :] += f32(cr[k])
        ys[k] = bf16(total[k, rows(ry_other, 32), CY])
        y1_send(k).start()

        @pl.when(ends)
        def _():
            zzs[k] = bf16(total[k, rows(rc, 64), CZ])
            zz_send(k).start()

    def stage2(k):
        @pl.when(inner)
        def _():
            zz_send(k).wait_recv()
            total[k, rows(rc, 64), CZ] += f32(zzr[k])
            mzs[k] = bf16(total[k, rows(rz_other, 32), CZ])
            mz_send(k).start()
            y1_send(k).wait_recv()
            total[k, rows(ry, 32), CY] += f32(yr[k])

        @pl.when(ends)
        def _():
            y1_send(k).wait_recv()
            zys[k] = bf16(total[k, rows(ry, 32), CY] + f32(yr[k]))
            zy_send(k).start()

    def stage3(k):
        @pl.when(inner)
        def _():
            mz_send(k).wait_recv()
            yzs[k] = bf16(total[k, rows(rz, 32), CZ] + f32(mzr[k]))
            yz_send(k).start()
            zy_send(k).wait_recv()
            mys[k] = bf16(total[k, rows(ry, 32), CY] + f32(zyr[k]))
            my_send(k).start()

    def stage4(k):
        @pl.when(inner)
        def _():
            yz_send(k).wait_recv()
            out[rows(rz, 32), col(k, 1)] = bf16(f32(yzs[k]) + f32(yzr[k]))
            final(FZM, k, 1, rz, mid).start()
            final(FZA, k, 1, rz, znb).start()
            final(SZ0, k, 1, rz, sib).start()
            my_send(k).wait_recv()
            out[rows(ry, 32), col(k, 0)] = bf16(f32(mys[k]) + f32(myr[k]))
            final(FYE, k, 0, ry, znb).start()
            final(FYY, k, 0, ry, ynb).start()
            final(SY0, k, 0, ry, sib).start()

    def stage5(k):
        @pl.when(inner)
        def _():
            final(FZM, k, 1, rz_other, mid).wait_recv()
            final(FZB, k, 1, rz_other, znb).start()
            final(SZ1, k, 1, rz_other, sib).start()
            final(FYY, k, 0, ry_other, ynb).wait_recv()
            final(SY1, k, 0, ry_other, sib).start()

        @pl.when(ends)
        def _():
            final(FZA, k, 1, rz, znb).wait_recv()
            final(SZ0, k, 1, rz, sib).start()
            final(FYE, k, 0, ry, znb).wait_recv()
            final(FYY, k, 0, ry, ynb).start()
            final(SY0, k, 0, ry, sib).start()

    def stage6(k):
        @pl.when(ends)
        def _():
            final(FZB, k, 1, rz_other, znb).wait_recv()
            final(SZ1, k, 1, rz_other, sib).start()
            final(FYY, k, 0, ry_other, ynb).wait_recv()
            final(SY1, k, 0, ry_other, sib).start()

    def at(k, fn):
        @pl.when(jnp.logical_and(k >= 0, k < n_chunks))
        def _():
            fn(k)

    @pl.loop(0, n_chunks + DELAYS[-1])
    def _(i):
        at(i - DELAYS[5], stage6)
        at(i - DELAYS[4], stage5)
        at(i - DELAYS[3], stage4)
        at(i - DELAYS[2], stage3)
        at(i - DELAYS[1], stage2)

        @pl.when(i < n_chunks)
        def _():
            fetch(i + kx * nb + SLOTS // 2 - 1)
            compute(i)

        at(i - DELAYS[0], stage1)

    rs, rs_y, rs_yo, rs_z, rs_zo = 64 - rc, 64 - rc + 32 * y, 64 - rc + 32 * (1 - y), 64 - rc + 32 * half, 64 - rc + 32 * (1 - half)

    @pl.loop(0, n_chunks)
    def _(k):
        final(SZ0, k, 1, rs_z, sib).wait_recv()
        final(SZ1, k, 1, rs_zo, sib).wait_recv()
        final(SY0, k, 0, rs_y, sib).wait_recv()
        final(SY1, k, 0, rs_yo, sib).wait_recv()
        core_send(k).wait_send()
        y1_send(k).wait_send()
        final(SZ0, k, 1, rz, sib).wait_send()
        final(SZ1, k, 1, rz_other, sib).wait_send()
        final(SY0, k, 0, ry, sib).wait_send()
        final(SY1, k, 0, ry_other, sib).wait_send()
        final(FYY, k, 0, ry, ynb).wait_send()

        @pl.when(inner)
        def _():
            mz_send(k).wait_send()
            my_send(k).wait_send()
            yz_send(k).wait_send()
            final(FYE, k, 0, ry, znb).wait_send()
            final(FZM, k, 1, rz, mid).wait_send()
            final(FZA, k, 1, rz, znb).wait_send()
            final(FZB, k, 1, rz_other, znb).wait_send()

        @pl.when(ends)
        def _():
            zz_send(k).wait_send()
            zy_send(k).wait_send()


DELAYS = (1, 3, 5, 7, 9, 11)


def mlp(x, wg, wu, wd):
    rows, d = x.shape
    ff = wg.shape[1]
    nc = d // (2 * TN)
    bf, f4 = jnp.bfloat16, jnp.float32
    any_spec = pl.BlockSpec(memory_space=pl.ANY)
    small = [pltpu.VMEM((nc, 32, TN), bf)] * 2
    return pl.pallas_call(
        kernel,
        out_shape=jax.ShapeDtypeStruct((rows, d), bf),
        in_specs=[any_spec] * 4,
        out_specs=pl.BlockSpec(memory_space=pltpu.VMEM),
        scratch_shapes=[
            pltpu.VMEM((rows, d), bf),
            pltpu.VMEM((SLOTS, TK, TN), bf),
            pltpu.VMEM((rows, TN), f4),
            pltpu.VMEM((rows, TN), f4),
            pltpu.VMEM((rows, ff), bf),
            pltpu.VMEM((nc, rows, 2 * TN), f4),
            pltpu.VMEM((nc, rows // 2, 2 * TN), bf),
            pltpu.VMEM((nc, rows // 2, 2 * TN), bf),
            *small,
            pltpu.VMEM((nc, rows // 2, TN), bf),
            pltpu.VMEM((nc, rows // 2, TN), bf),
            *small,
            *small,
            *small,
            *small,
            pltpu.SemaphoreType.DMA((d // TK,)),
            pltpu.SemaphoreType.DMA((SLOTS,)),
            pltpu.SemaphoreType.DMA((16, nc)),
            pltpu.SemaphoreType.DMA((16, nc)),
        ],
        compiler_params=pltpu.CompilerParams(
            collective_id=0, has_side_effects=True, vmem_limit_bytes=60 << 20),
        cost_estimate=pl.CostEstimate(
            flops=6 * rows * d * ff, bytes_accessed=6 * d * ff, transcendentals=rows * ff),
    )(x, wg, wu, wd)


def solution(mesh):
    return jax.shard_map(
        mlp,
        mesh=mesh,
        in_specs=(P("dp", None), P(None, "tp"), P(None, "tp"), P("tp", None)),
        out_specs=P("dp", None),
        check_vma=False,
    )
```

time: 156 us -> 67.4 us (0.43)
  waiting for transfers between devices: 101 us -> 0 us
  Pallas kernels: 0 us -> 64.1 us
  matrix products: 37.4 us -> 0 us
  between operations: 13.4 us -> 0.01 us
  local copies, waits for them, and re-layouts: 4.68 us -> 3.1 us
    psum x1 -> x0, waiting for transfers between devices: 101 us -> none  [step(): return lax.psum(term, 'tp')]
    pallas_call x0 -> x1, Pallas kernels: none -> 64.1 us  [mlp(): pl.pallas_call(kernel, out_shape=jax.ShapeDtypeStruct((rows, d), bf), in_...]
    dot_general x2 -> x0, matrix products: 37.4 us -> none  [the longest x1 24.5 us: step(): jnp.dot(hidden, w_down, preferred_element_type=jnp.float32)]
    unnamed x3 -> x1, local copies, waits for them, and re-layouts: 4.68 us -> 3.1 us
  transfers between devices with their start and end apart: 1 -> 0, of which waited for: 1 -> 0; matrix products, arithmetic and copies ran while one was open for 0% -> 0% of each run, Pallas kernels for 0% -> 0%
where the time goes in v1:
time: 67.4 us; the launch traced here: 67.3 us
  Pallas kernels  64.1 us (95%)
  local copies, waits for them, and re-layouts  3.1 us (5%)
    pallas_call x1, Pallas kernels, mlp(): pl.pallas_call(kernel, out_shape=jax.ShapeDtypeStruct((rows, d), bf), in_...  64.1 us
    unnamed x1, local copies, waits for them, and re-layouts  3.1 us

profile of v1, /device:TPU:0, one launch (start us, length us, event | category | flops | bytes accessed | tf_op | source)
XLA Modules:
  0.0 67.3 jit_solution(13468023358408871502)
XLA Ops:
  0.0 64.1 %shard_map.46 = bf16[128,8192]{1,0:T(8,128)(2,1)} custom-call(bf16[128,8192]{1,0:T(8,128)(2,1)} %x_hbm.1, bf16[8192,2048]{1,0:T(8,128)(2,1)} %wg_hbm.1, bf16[8192,2048]{1,0:T(8,128)(2,1)} %wu_hbm.1, bf16[2048,8192]{1,0:T(8,128)(2,1)} %wd_hbm.1), custom_call_target="tpu_custom_call" | custom-call | flops 12884901888 | bytes 100663296 | tf_op jit(solution)/shard_map/pallas_call | solution.py:322
  64.2 3.1 %copy.6 = bf16[128,8192]{1,0:T(8,128)(2,1)} copy(bf16[128,8192]{1,0:T(8,128)(2,1)} %shard_map.46) | data formatting | bytes 4194304
